TPU v7x, 32 devices: a whole 2x2x4 slice. The times are simulated.
32 devices in a mesh: clip: 2 (over y), ha: 8 (over z, x), ta: 2 (over core).
Axes of the slice: x: 2, y: 2, z: 4, core: 2. Of those that a mesh axis runs over, the one named last changes fastest.
Arguments:
- latent_tokens: bfloat16 [16, 512, 64], P('clip', ('ha', 'ta')), parts along dimension 0, may hold values from -8 to 8
- w_in: bfloat16 [3, 3, 3, 16, 384], replicated, may hold values from -0.3125 to 0.3125
- b_in: float32 [384], replicated, may hold values from -3 to 3
- gn_gain: float32 [384], replicated, may hold values from 0.1 to 1.9
- gn_shift: float32 [384], replicated, may hold values from -3 to 3
- w_mid: bfloat16 [3, 3, 3, 384, 384], replicated, may hold values from -0.109375 to 0.109375
- b_mid: float32 [384], replicated, may hold values from -3 to 3
Outputs:
- decoded: bfloat16 [16, 16, 128, 384], P(('clip', 'ta'), 'ha'), parts along dimension 0
There are 2 independent parts, one for each index of `clip`. A program takes and returns all parts, laid end to end along the dimension named above; an argument that names none is the same for every part. Nothing has to cross between parts.
All inputs are finite; a program needn't handle non-finite values.
Results may differ from a plain program's by a relative error of at most 0.0054.
Values may be sent and summed in bfloat16 or wider, within the bound.
A program may use at most 64 MiB of HBM per device.

v0:
```python
import jax
import jax.numpy as jnp
from jax import lax
from jax.sharding import PartitionSpec as P

GROUPS = 32
H_DEV = 2
W = 128
eps = 1e-06


def passed_along(value, axis, by):
    devices = lax.axis_size(axis)
    pairs = [(i, i + by) for i in range(devices) if 0 <= i + by < devices]
    return lax.ppermute(value, axis, pairs)


def extended_2(value, sides, width):
    for axis, dim in sides:
        devices, length = (lax.axis_size(axis), value.shape[dim])
        up = [(i, (i + 1) % devices) for i in range(devices - 1)]
        down = [(j, i) for i, j in up]
        last = lax.slice_in_dim(value, length - width, length, axis=dim)
        first = lax.slice_in_dim(value, 0, width, axis=dim)
        before = lax.ppermute(last, axis, up)
        after = lax.ppermute(first, axis, down)
        value = jnp.concatenate([before, value, after], axis=dim)
    return value


def unpatch(tokens, rows, cols):
    frames = tokens.shape[0]
    latent_ch = tokens.shape[2] // 4
    blocks = tokens.reshape(frames, rows // 2, cols // 2, 2, 2, latent_ch)
    return blocks.transpose(0, 1, 3, 2, 4, 5).reshape(frames, rows, cols, latent_ch)


def pad_cols(field):
    return jnp.pad(field, ((0, 0), (0, 0), (1, 1), (0, 0)))


def input_conv(padded, w_in, b_in, frames, rows, cols):
    pieces = [
        padded[frame_tap : frame_tap + frames, row_tap : row_tap + rows, col_tap : col_tap + cols]
        for frame_tap in range(3)
        for row_tap in range(3)
        for col_tap in range(3)
    ]
    stacked = jnp.concatenate(pieces, axis=-1).reshape(frames * rows * cols, -1)
    result = jnp.dot(
        stacked, w_in.reshape(stacked.shape[1], -1), preferred_element_type=jnp.float32
    )
    return (result + b_in).reshape(frames, rows, cols, -1)


def middle_conv(padded, w_mid, frames, rows, cols):
    channels = padded.shape[-1]
    total = jnp.zeros((frames * rows * cols, w_mid.shape[-1]), jnp.float32)
    for frame_tap in range(3):
        for row_tap in range(3):
            slab = jnp.concatenate(
                [
                    padded[
                        frame_tap : frame_tap + frames,
                        row_tap : row_tap + rows,
                        col_tap : col_tap + cols,
                    ]
                    for col_tap in range(3)
                ],
                axis=-1,
            ).reshape(frames * rows * cols, 3 * channels)
            total = total + jnp.dot(
                slab,
                w_mid[frame_tap, row_tap].reshape(3 * channels, -1),
                preferred_element_type=jnp.float32,
            )
    return total.reshape(frames, rows, cols, -1)


def group_totals(field):
    grouped = field.reshape(-1, GROUPS, field.shape[-1] // GROUPS)
    return jnp.sum(grouped, axis=(0, 2))


def normalize(hidden, mean, var, gn_gain, gn_shift):
    members = hidden.shape[-1] // GROUPS
    mean_chan = jnp.repeat(mean, members)
    scale_chan = jnp.repeat(lax.rsqrt(var + eps), members)
    scaled = (hidden.astype(jnp.float32) - mean_chan) * scale_chan * gn_gain + gn_shift
    return jax.nn.silu(scaled).astype(jnp.bfloat16)


def body(latent_tokens, w_in, b_in, gn_gain, gn_shift, w_mid, b_mid):
    rows = H_DEV
    cols = W
    moved = lax.all_to_all(latent_tokens, "ta", split_axis=0, concat_axis=1, tiled=True)
    latent = unpatch(moved, rows, cols)
    frames = latent.shape[0]
    earlier = passed_along(latent, "ta", 1)
    extended = jnp.concatenate([earlier, latent], axis=0)
    framed = extended_2(extended, (("ha", 1),), 2)
    wide_hidden = input_conv(pad_cols(framed), w_in, b_in, frames + 2, rows + 2, cols).astype(
        jnp.bfloat16
    )
    hidden = wide_hidden[2:, 1 : rows + 1]
    values = lax.optimization_barrier(hidden).astype(jnp.float32)
    members = values.shape[-1] // GROUPS
    count = float(lax.axis_size("ha") * lax.axis_size("ta") * frames * rows * cols * members)
    mean = lax.psum(group_totals(values), ("ha", "ta")) / count
    centered = values - jnp.repeat(mean, members)
    var = lax.psum(group_totals(centered * centered), ("ha", "ta")) / count
    active = normalize(wide_hidden, mean, var, gn_gain, gn_shift)
    frame_pos = lax.axis_index("ta") * frames + jnp.arange(frames + 2, dtype=jnp.int32) - 2
    row_pos = lax.axis_index("ha") * rows + jnp.arange(rows + 2, dtype=jnp.int32) - 1
    inside = (
        (frame_pos >= 0)[:, None]
        & (row_pos >= 0)[None, :]
        & (row_pos < rows * lax.axis_size("ha"))[None, :]
    )
    padded = jnp.where(inside[:, :, None, None], active, jnp.zeros_like(active))
    branch = middle_conv(pad_cols(padded), w_mid, frames, rows, cols)
    return (values + branch + b_mid).astype(jnp.bfloat16)


def solution(mesh):
    placed = (P("clip", ("ha", "ta"), None), P(), P(), P(), P(), P(), P())
    return jax.shard_map(
        body,
        mesh=mesh,
        in_specs=placed,
        out_specs=P(("clip", "ta"), "ha", None, None),
        check_vma=False,
    )
```

profile of v0, /device:TPU:0, one launch (start us, length us, event | category | flops | bytes accessed | tf_op | source)
XLA Modules:
  0.0 131.4 jit_solution(58256040233946923)
XLA Ops:
  0.0 1.0 reshape.124
  1.0 3.7 %all_to_all.15 = bf16[2,2,4096]{2,1,0:T(2,128)(2,1)S(1)} all-to-all(bf16[2,2,4096]{2,1,0:T(2,128)(2,1)S(1)} %reshape.124), channel_id=1, replica_groups=mesh['clip'=2,'ha'=8,'ta'=2] {'ta'}, dimensions={0} | all-to-all | bytes 65536 | tf_op jit(solution)/shard_map/all_to_all | solution.py:96
  4.8 0.1 reshape.125
  4.9 0.1 copy.14
  5.0 0.1 reshape.110
  5.1 0.2 copy.15
  5.3 2.1 %collective-permute-start = (bf16[4,2,128,16]{3,2,1,0:T(8,128)(2,1)S(1)}, bf16[4,2,128,16]{3,2,1,0:T(8,128)(2,1)S(1)}, u32[]{:S(2)}, u32[]{:S(2)}) collective-permute-start(bf16[4,2,128,16]{3,2,1,0:T(8,128)(2,1)S(1)} %bitcast.63), channel_id=1, source_target_pairs={{0,1},{2,3},{4,5},{6,7},{8,9},{10,11},{12,13},{14,15},{16,17},{18,... | collective-permute-start | bytes 98312 | tf_op jit(solution)/shard_map/ppermute | solution.py:15
  7.4 5.7 %fusion.25 = (bf16[1,1,3,384,384]{4,3,2,1,0:T(8,128)(2,1)}, bf16[1,1,3,384,384]{4,3,2,1,0:T(8,128)(2,1)}, bf16[1,1,3,384,384]{4,3,2,1,0:T(8,128)(2,1)}, bf16[1,1...) fusion(bf16[3,3,3,384,384]{4,3,2,1,0:T(8,128)(2,1)} %param.12), kind=kLoop, calls=%fused_computation.94 | loop fusion | bytes 15925248 | tf_op jit(solution)/shard_map/slice | solution.py:74
  13.2 0.1 copy.17
  13.3 0.1 copy.16
  13.4 1.3 collective-permute-start.2
  14.7 5.5 %collective-permute-start.1 = (bf16[8,2,128,16]{2,3,1,0:T(8,128)(2,1)S(1)}, bf16[8,2,128,16]{2,3,1,0:T(8,128)(2,1)S(1)}, u32[]{:S(2)}, u32[]{:S(2)}) collective-permute-start(bf16[8,2,128,16]{2,3,1,0:T(8,128)(2,1)S(1)} %pad_maximum_fusion.11), channel_id=1, source_target_pairs={{0,2},{2,4},{4,6},{6,8},{8,10},{10,12},{12,14},{1,3},{3,5},{5,7},{... | collective-permute-start | bytes 196616 | tf_op jit(solution)/shard_map/ppermute | solution.py:25
  20.3 0.2 collective-permute-done.2
  20.6 1.6 %collective-permute-done.1 = bf16[8,2,128,16]{2,3,1,0:T(8,128)(2,1)S(1)} collective-permute-done((bf16[8,2,128,16]{2,3,1,0:T(8,128)(2,1)S(1)}, bf16[8,2,128,16]{2,3,1,0:T(8,128)(2,1)S(1)}, u32[]{:S(2)}, u32[]{:S(2)}) %collective-permute-start.1) | collective-permute-done | bytes 65568 | tf_op jit(solution)/shard_map/ppermute | solution.py:25
  22.3 0.1 fusion.6
  22.4 0.1 fusion.7
  22.6 0.1 fusion.8
  22.7 0.1 fusion.9
  23.4 0.1 fusion.14
  23.7 0.1 fusion.17
  24.0 0.1 fusion.19
  24.4 0.1 fusion.22
  24.5 1.0 copy.18
  25.6 3.2 %reshape.112 = bf16[3072,432]{0,1:T(8,128)(2,1)} reshape(bf16[6,4,128,432]{2,1,0,3:T(4,128)(2,1)S(1)} %copy.18) | data formatting | bytes 5308416 | tf_op jit(solution)/shard_map/reshape | solution.py:49
  28.7 3.6 %add_convert_fusion = bf16[3072,384]{1,0:T(8,128)(2,1)S(1)} fusion(bf16[3072,432]{0,1:T(8,128)(2,1)} %reshape.112, bf16[432,384]{1,0:T(8,128)(2,1)S(1)} %bitcast.49, f32[384]{0:T(512)S(1)} %copy-done.14), kind=kOutput, calls=%fused_computation.1 | convolution fusion | flops 1021575168 | bytes 5346816 | tf_op jit(solution)/shard_map/dot_general | solution.py:50
  32.4 0.2 convert_reduce_fusion
  32.7 0.1 reduce_sum.25
  32.8 32.9 %psum.14 = f32[32]{0:T(128)S(1)} all-reduce(f32[32]{0:T(128)S(1)} %reduce_sum.25), channel_id=1, replica_groups=mesh['clip'=2,'ha'=8,'ta'=2] {'ha','ta'}, use_global_device_ids=true, to_apply=%region_2.3 | all-reduce | flops 32 | bytes 256 | tf_op jit(solution)/shard_map/psum | solution.py:109
  66.0 0.3 fusion.2
  66.4 0.1 reduce_sum.37
  66.5 29.7 %psum.15 = f32[32]{0:T(128)S(1)} all-reduce(f32[32]{0:T(128)S(1)} %reduce_sum.37), channel_id=1, replica_groups=mesh['clip'=2,'ha'=8,'ta'=2] {'ha','ta'}, use_global_device_ids=true, to_apply=%region_5.6 | all-reduce | flops 32 | bytes 256 | tf_op jit(solution)/shard_map/psum | solution.py:111
  96.2 0.1 mul.34
  96.4 1.9 %fusion = bf16[6,4,128,384]{3,2,1,0:T(8,128)(2,1)S(1)} fusion(bf16[6,4,128,384]{3,2,1,0:T(8,128)(2,1)S(1)} %bitcast.53, f32[384]{0:T(512)S(1)} %copy-done.11, f32[384]{0:T(512)S(1)} %copy-done.12, f32[384]{0:T(512)S(1)} %mul.34, f32[384]{0:T(512)S(1)} %sub.26, pred[6,4]{1,0:T(8,128)(4,1)S(1)} %and_and_fusion), kind=kLoop, calls=%fused_computation.5 | loop fusion | flops 12976128 | bytes 4724760 | tf_op jit(solution)/shard_map/jit(_where)/select_n | solution.py:120
  98.3 3.6 %pad_slice_fusion.18 = (bf16[4,2,128,384]{3,2,1,0:T(8,128)(2,1)S(1)}, bf16[4,2,128,384]{3,2,1,0:T(8,128)(2,1)S(1)}, bf16[4,2,128,384]{3,2,1,0:T(8,128)(2,1)S(1)}...) fusion(bf16[6,4,128,384]{3,2,1,0:T(8,128)(2,1)S(1)} %fusion), kind=kLoop, calls=%fused_computation.76 | loop fusion | bytes 13369344 | tf_op jit(solution)/shard_map/slice | solution.py:63
  101.9 0.7 fusion.26
  102.6 3.8 %pad_slice_fusion.19 = (bf16[4,2,128,384]{3,2,1,0:T(8,128)(2,1)S(1)}, bf16[4,2,128,384]{3,2,1,0:T(8,128)(2,1)S(1)}, bf16[4,2,128,384]{3,2,1,0:T(8,128)(2,1)S(1)}...) fusion(bf16[6,4,128,384]{3,2,1,0:T(8,128)(2,1)S(1)} %fusion), kind=kLoop, calls=%fused_computation.77 | loop fusion | bytes 11010048 | tf_op jit(solution)/shard_map/slice | solution.py:63
  106.4 0.3 pad_maximum_fusion.7
  106.7 0.9 copy-done.10
  107.6 1.4 %fusion.34 = f32[1024,384]{1,0:T(8,128)S(1)} fusion(bf16[1024,1152]{1,0:T(8,128)(2,1)S(1)} %bitcast.55, bf16[1152,384]{1,0:T(8,128)(2,1)S(1)} %bitcast.72), kind=kOutput, calls=%fused_computation.103 | convolution fusion | flops 905969664 | bytes 4816896 | tf_op jit(solution)/shard_map/dot_general | solution.py:72
  109.0 0.3 pad_maximum_fusion.6
  109.3 0.9 copy-done.9
  110.2 1.4 %fusion.33 = f32[1024,384]{1,0:T(8,128)S(1)} fusion(bf16[1024,1152]{1,0:T(8,128)(2,1)S(1)} %bitcast.56, bf16[1152,384]{1,0:T(8,128)(2,1)S(1)} %bitcast.71), kind=kOutput, calls=%fused_computation.102 | convolution fusion | flops 905969664 | bytes 4816896 | tf_op jit(solution)/shard_map/dot_general | solution.py:72
  111.6 0.3 pad_maximum_fusion.5
  111.9 0.9 copy-done.8
  112.8 1.4 %fusion.32 = f32[1024,384]{1,0:T(8,128)S(1)} fusion(bf16[1024,1152]{1,0:T(8,128)(2,1)S(1)} %bitcast.57, bf16[1152,384]{1,0:T(8,128)(2,1)S(1)} %bitcast.70), kind=kOutput, calls=%fused_computation.101 | convolution fusion | flops 905969664 | bytes 4816896 | tf_op jit(solution)/shard_map/dot_general | solution.py:72
  114.2 0.3 pad_maximum_fusion.4
  114.5 0.9 copy-done.7
  115.4 1.4 %fusion.31 = f32[1024,384]{1,0:T(8,128)S(1)} fusion(bf16[1024,1152]{1,0:T(8,128)(2,1)S(1)} %bitcast.58, bf16[1152,384]{1,0:T(8,128)(2,1)S(1)} %bitcast.69), kind=kOutput, calls=%fused_computation.100 | convolution fusion | flops 905969664 | bytes 4816896 | tf_op jit(solution)/shard_map/dot_general | solution.py:72
  116.9 0.3 pad_maximum_fusion.3
  117.2 0.9 copy-done.6
  118.0 1.4 %fusion.30 = f32[1024,384]{1,0:T(8,128)S(1)} fusion(bf16[1024,1152]{1,0:T(8,128)(2,1)S(1)} %bitcast.59, bf16[1152,384]{1,0:T(8,128)(2,1)S(1)} %bitcast.68), kind=kOutput, calls=%fused_computation.99 | convolution fusion | flops 905969664 | bytes 4816896 | tf_op jit(solution)/shard_map/dot_general | solution.py:72
  119.5 0.3 pad_maximum_fusion.2
  119.8 0.9 copy-done.5
  120.6 1.4 %fusion.29 = f32[1024,384]{1,0:T(8,128)S(1)} fusion(bf16[1024,1152]{1,0:T(8,128)(2,1)S(1)} %bitcast.60, bf16[1152,384]{1,0:T(8,128)(2,1)S(1)} %bitcast.67), kind=kOutput, calls=%fused_computation.98 | convolution fusion | flops 905969664 | bytes 4816896 | tf_op jit(solution)/shard_map/dot_general | solution.py:72
  122.1 0.3 pad_maximum_fusion
  122.4 0.9 copy-done.4
  123.2 1.4 %fusion.27 = f32[1024,384]{1,0:T(8,128)S(1)} fusion(bf16[1024,1152]{1,0:T(8,128)(2,1)S(1)} %bitcast.61, bf16[1152,384]{1,0:T(8,128)(2,1)S(1)} %bitcast.66), kind=kOutput, calls=%fused_computation.96 | convolution fusion | flops 905969664 | bytes 4816896 | tf_op jit(solution)/shard_map/dot_general | solution.py:72
  124.7 0.3 pad_maximum_fusion.1
  125.0 0.9 copy-done.3
  125.8 1.4 %fusion.28 = f32[1024,384]{1,0:T(8,128)S(1)} fusion(bf16[1024,1152]{1,0:T(8,128)(2,1)S(1)} %bitcast.62, bf16[1152,384]{1,0:T(8,128)(2,1)S(1)} %bitcast.65), kind=kOutput, calls=%fused_computation.97 | convolution fusion | flops 905969664 | bytes 4816896 | tf_op jit(solution)/shard_map/dot_general | solution.py:72
  127.3 0.3 pad_maximum_fusion.8
  127.6 0.9 copy-done.2
  128.5 1.7 %add_add_fusion = f32[1024,384]{1,0:T(8,128)S(1)} fusion(f32[1024,384]{1,0:T(8,128)S(1)} %fusion.34, f32[1024,384]{1,0:T(8,128)S(1)} %fusion.33, f32[1024,384]{1,0:T(8,128)S(1)} %fusion.32, f32[1024,384]{1,0:T(8,128)S(1)} %fusion.31, f32[1024,384]{1,0:T(8,128)S(1)} %fusion.30, f32[1024,384]{1,0:T(8,128)S(1)} %fusion.29, f32[1024,384]{1,0:T(8,128)S(1)} %fusion.27, ...), kind=kOutput, calls=%fused_computation.19 | convolution fusion | flops 909115392 | bytes 17399808 | tf_op jit(solution)/shard_map/dot_general | solution.py:72
  130.2 1.1 fusion.4
  (55 shorter events, 2.0 us)
Async XLA Ops:
  0.0 28.7 %copy-start = (bf16[3,3,3,16,384]{4,3,2,1,0:T(8,128)(2,1)S(1)}, bf16[3,3,3,16,384]{4,3,2,1,0:T(8,128)(2,1)}, u32[]{:S(2)}) copy-start(bf16[3,3,3,16,384]{4,3,2,1,0:T(8,128)(2,1)} %param.8) | copy-start | bytes 995332
  5.3 8.0 %collective-permute-start = (bf16[4,2,128,16]{3,2,1,0:T(8,128)(2,1)S(1)}, bf16[4,2,128,16]{3,2,1,0:T(8,128)(2,1)S(1)}, u32[]{:S(2)}, u32[]{:S(2)}) collective-permute-start(bf16[4,2,128,16]{3,2,1,0:T(8,128)(2,1)S(1)} %bitcast.63), channel_id=1, source_target_pairs={{0,1},{2,3},{4,5},{6,7},{8,9},{10,11},{12,13},{14,15},{16,17},{18,... | collective-permute-start | bytes 98312 | tf_op jit(solution)/shard_map/ppermute | solution.py:15
  13.4 7.1 %collective-permute-start.2 = (bf16[8,2,128,16]{2,3,1,0:T(8,128)(2,1)S(1)}, bf16[8,2,128,16]{2,3,1,0:T(8,128)(2,1)S(1)}, u32[]{:S(2)}, u32[]{:S(2)}) collective-permute-start(bf16[8,2,128,16]{2,3,1,0:T(8,128)(2,1)S(1)} %pad_maximum_fusion.11), channel_id=1, source_target_pairs={{2,0},{4,2},{6,4},{8,6},{10,8},{12,10},{14,12},{3,1},{5,3},{7,5},{... | collective-permute-start | bytes 196616 | tf_op jit(solution)/shard_map/ppermute | solution.py:26
  14.7 7.4 %collective-permute-start.1 = (bf16[8,2,128,16]{2,3,1,0:T(8,128)(2,1)S(1)}, bf16[8,2,128,16]{2,3,1,0:T(8,128)(2,1)S(1)}, u32[]{:S(2)}, u32[]{:S(2)}) collective-permute-start(bf16[8,2,128,16]{2,3,1,0:T(8,128)(2,1)S(1)} %pad_maximum_fusion.11), channel_id=1, source_target_pairs={{0,2},{2,4},{4,6},{6,8},{8,10},{10,12},{12,14},{1,3},{3,5},{5,7},{... | collective-permute-start | bytes 196616 | tf_op jit(solution)/shard_map/ppermute | solution.py:25
  25.5 3.2 %copy-start.14 = (f32[384]{0:T(512)S(1)}, f32[384]{0:T(512)}, u32[]{:S(2)}) copy-start(f32[384]{0:T(512)} %param.9) | copy-start | bytes 4612
  32.3 64.0 %copy-start.11 = (f32[384]{0:T(512)S(1)}, f32[384]{0:T(512)}, u32[]{:S(2)}) copy-start(f32[384]{0:T(512)} %param.11) | copy-start | bytes 4612
  32.3 64.0 %copy-start.12 = (f32[384]{0:T(512)S(1)}, f32[384]{0:T(512)}, u32[]{:S(2)}) copy-start(f32[384]{0:T(512)} %param.10) | copy-start | bytes 4612
  106.4 1.2 copy-start.10
  109.0 1.2 copy-start.9
  111.6 1.2 copy-start.8
  114.2 1.2 copy-start.7
  116.8 1.2 copy-start.6
  119.5 1.2 copy-start.5
  122.1 1.2 copy-start.4
  124.7 1.2 copy-start.3
  127.3 1.2 copy-start.2
  128.5 1.8 %copy-start.13 = (f32[384]{0:T(512)S(1)}, f32[384]{0:T(512)}, u32[]{:S(2)}) copy-start(f32[384]{0:T(512)} %param.13) | copy-start | bytes 4612
  128.5 2.9 %copy-start.1 = (bf16[3,3,3,16,384]{4,3,2,1,0:T(8,128)(2,1)S(1)}, bf16[3,3,3,16,384]{4,3,2,1,0:T(8,128)(2,1)}, u32[]{:S(2)}) copy-start(bf16[3,3,3,16,384]{4,3,2,1,0:T(8,128)(2,1)} %param.8) | copy-start | bytes 995332
where the time goes:
time: 132 us; the launch traced here: 131 us
  blocking collectives  66.4 us (50%)
  local copies, waits for them, and re-layouts  30.3 us (23%)
  matrix products  16.8 us (13%)
  starting transfers between devices  8.88 us (7%)
  other arithmetic  6.55 us (5%)
  waiting for transfers between devices  1.81 us (1%)
    psum x1, blocking collectives, body(): mean = lax.psum(group_totals(values), ('ha', 'ta')) / count  32.9 us
    psum x1, blocking collectives, body(): var = lax.psum(group_totals(centered * centered), ('ha', 'ta')) / count  29.7 us
    dot_general x9, matrix products, middle_conv(): jnp.dot(slab, w_mid[frame_tap, row_tap].reshape(3 * channels, -1), prefer...  13.2 us
    unnamed x58, local copies, waits for them, and re-layouts  10.8 us
    slice x3, local copies, waits for them, and re-layouts, middle_conv(): padded[frame_tap:frame_tap + frames, row_tap:row_tap + rows, col_tap:col_...  8.12 us
    slice x1, local copies, waits for them, and re-layouts, middle_conv(): w_mid[frame_tap, row_tap].reshape(3 * channels, -1)  5.75 us
    ppermute x1, starting transfers between devices, extended_2(): before = lax.ppermute(last, axis, up)  5.5 us
    all_to_all x1, blocking collectives, body(): lax.all_to_all(latent_tokens, 'ta', split_axis=0, concat_axis=1, tiled=True)  3.75 us
  transfers between devices with their start and end apart: 3, of which 2 were waited for; matrix products, arithmetic and copies ran while one was open for 5% of the time, Pallas kernels for 0%

commit v1 on v0

--- a/solution.py
+++ b/solution.py
@@ -108,7 +108,7 @@
     count = float(lax.axis_size("ha") * lax.axis_size("ta") * frames * rows * cols * members)
     mean = lax.psum(group_totals(values), ("ha", "ta")) / count
     centered = values - jnp.repeat(mean, members)
-    var = lax.psum(group_totals(centered * centered), ("ha", "ta")) / count
+    var = lax.psum(lax.psum(group_totals(centered * centered), "ha"), "ta") / count
     active = normalize(wide_hidden, mean, var, gn_gain, gn_shift)
     frame_pos = lax.axis_index("ta") * frames + jnp.arange(frames + 2, dtype=jnp.int32) - 2
     row_pos = lax.axis_index("ha") * rows + jnp.arange(rows + 2, dtype=jnp.int32) - 1

time: 132 us -> 122 us (0.924)
  blocking collectives: 66.4 us -> 56.5 us
    psum x1 -> x2, blocking collectives: 29.7 us -> 19.8 us  [the longest x1 17.1 us: body(): lax.psum(group_totals(centered * centered), 'ha')]
where the time goes in v1:
time: 122 us; the launch traced here: 121 us
  blocking collectives  56.5 us (46%)
  local copies, waits for them, and re-layouts  30.3 us (25%)
  matrix products  16.8 us (14%)
  starting transfers between devices  8.88 us (7%)
  other arithmetic  6.55 us (5%)
  waiting for transfers between devices  1.81 us (1%)
    psum x1, blocking collectives, body(): mean = lax.psum(group_totals(values), ('ha', 'ta')) / count  32.9 us
    psum x1, blocking collectives, body(): lax.psum(group_totals(centered * centered), 'ha')  17.1 us
    dot_general x9, matrix products, middle_conv(): jnp.dot(slab, w_mid[frame_tap, row_tap].reshape(3 * channels, -1), prefer...  13.2 us
    unnamed x58, local copies, waits for them, and re-layouts  10.8 us
    slice x3, local copies, waits for them, and re-layouts, middle_conv(): padded[frame_tap:frame_tap + frames, row_tap:row_tap + rows, col_tap:col_...  8.12 us
    slice x1, local copies, waits for them, and re-layouts, middle_conv(): w_mid[frame_tap, row_tap].reshape(3 * channels, -1)  5.74 us
    ppermute x1, starting transfers between devices, extended_2(): before = lax.ppermute(last, axis, up)  5.5 us
    all_to_all x1, blocking collectives, body(): lax.all_to_all(latent_tokens, 'ta', split_axis=0, concat_axis=1, tiled=True)  3.75 us
  transfers between devices with their start and end apart: 3, of which 2 were waited for; matrix products, arithmetic and copies ran while one was open for 5% of the time, Pallas kernels for 0%

profile of v1, /device:TPU:0, one launch (start us, length us, event | category | flops | bytes accessed | tf_op | source)
XLA Modules:
  0.0 121.4 jit_solution(8321062573476424104)
XLA Ops:
  0.0 1.0 reshape.124
  1.0 3.7 %all_to_all.15 = bf16[2,2,4096]{2,1,0:T(2,128)(2,1)S(1)} all-to-all(bf16[2,2,4096]{2,1,0:T(2,128)(2,1)S(1)} %reshape.124), channel_id=1, replica_groups=mesh['clip'=2,'ha'=8,'ta'=2] {'ta'}, dimensions={0} | all-to-all | bytes 65536 | tf_op jit(solution)/shard_map/all_to_all | solution.py:96
  4.8 0.1 reshape.125
  4.9 0.1 copy.14
  5.0 0.1 reshape.110
  5.1 0.2 copy.15
  5.3 2.1 %collective-permute-start = (bf16[4,2,128,16]{3,2,1,0:T(8,128)(2,1)S(1)}, bf16[4,2,128,16]{3,2,1,0:T(8,128)(2,1)S(1)}, u32[]{:S(2)}, u32[]{:S(2)}) collective-permute-start(bf16[4,2,128,16]{3,2,1,0:T(8,128)(2,1)S(1)} %bitcast.63), channel_id=1, source_target_pairs={{0,1},{2,3},{4,5},{6,7},{8,9},{10,11},{12,13},{14,15},{16,17},{18,... | collective-permute-start | bytes 98312 | tf_op jit(solution)/shard_map/ppermute | solution.py:15
  7.4 5.7 %fusion.25 = (bf16[1,1,3,384,384]{4,3,2,1,0:T(8,128)(2,1)}, bf16[1,1,3,384,384]{4,3,2,1,0:T(8,128)(2,1)}, bf16[1,1,3,384,384]{4,3,2,1,0:T(8,128)(2,1)}, bf16[1,1...) fusion(bf16[3,3,3,384,384]{4,3,2,1,0:T(8,128)(2,1)} %param.12), kind=kLoop, calls=%fused_computation.94 | loop fusion | bytes 15925248 | tf_op jit(solution)/shard_map/slice | solution.py:74
  13.2 0.1 copy.17
  13.3 0.1 copy.16
  13.4 1.3 %collective-permute-start.2 = (bf16[8,2,128,16]{2,3,1,0:T(8,128)(2,1)S(1)}, bf16[8,2,128,16]{2,3,1,0:T(8,128)(2,1)S(1)}, u32[]{:S(2)}, u32[]{:S(2)}) collective-permute-start(bf16[8,2,128,16]{2,3,1,0:T(8,128)(2,1)S(1)} %pad_maximum_fusion.11), channel_id=1, source_target_pairs={{2,0},{4,2},{6,4},{8,6},{10,8},{12,10},{14,12},{3,1},{5,3},{7,5},{... | collective-permute-start | bytes 196616 | tf_op jit(solution)/shard_map/ppermute | solution.py:26
  14.7 5.5 %collective-permute-start.1 = (bf16[8,2,128,16]{2,3,1,0:T(8,128)(2,1)S(1)}, bf16[8,2,128,16]{2,3,1,0:T(8,128)(2,1)S(1)}, u32[]{:S(2)}, u32[]{:S(2)}) collective-permute-start(bf16[8,2,128,16]{2,3,1,0:T(8,128)(2,1)S(1)} %pad_maximum_fusion.11), channel_id=1, source_target_pairs={{0,2},{2,4},{4,6},{6,8},{8,10},{10,12},{12,14},{1,3},{3,5},{5,7},{... | collective-permute-start | bytes 196616 | tf_op jit(solution)/shard_map/ppermute | solution.py:25
  20.3 0.2 collective-permute-done.2
  20.6 1.6 %collective-permute-done.1 = bf16[8,2,128,16]{2,3,1,0:T(8,128)(2,1)S(1)} collective-permute-done((bf16[8,2,128,16]{2,3,1,0:T(8,128)(2,1)S(1)}, bf16[8,2,128,16]{2,3,1,0:T(8,128)(2,1)S(1)}, u32[]{:S(2)}, u32[]{:S(2)}) %collective-permute-start.1) | collective-permute-done | bytes 65568 | tf_op jit(solution)/shard_map/ppermute | solution.py:25
  22.3 0.1 fusion.6
  22.4 0.1 fusion.7
  22.7 0.1 fusion.9
  23.3 0.1 fusion.14
  23.7 0.1 fusion.17
  24.0 0.1 fusion.19
  24.4 0.1 fusion.22
  24.5 1.0 copy.18
  25.5 3.1 %reshape.112 = bf16[3072,432]{0,1:T(8,128)(2,1)} reshape(bf16[6,4,128,432]{2,1,0,3:T(4,128)(2,1)S(1)} %copy.18) | data formatting | bytes 5308416 | tf_op jit(solution)/shard_map/reshape | solution.py:49
  28.7 3.6 %add_convert_fusion = bf16[3072,384]{1,0:T(8,128)(2,1)S(1)} fusion(bf16[3072,432]{0,1:T(8,128)(2,1)} %reshape.112, bf16[432,384]{1,0:T(8,128)(2,1)S(1)} %bitcast.49, f32[384]{0:T(512)S(1)} %copy-done.14), kind=kOutput, calls=%fused_computation.1 | convolution fusion | flops 1021575168 | bytes 5346816 | tf_op jit(solution)/shard_map/dot_general | solution.py:50
  32.4 0.2 convert_reduce_fusion
  32.7 0.1 reduce_sum.25
  32.8 32.9 %psum.21 = f32[32]{0:T(128)S(1)} all-reduce(f32[32]{0:T(128)S(1)} %reduce_sum.25), channel_id=1, replica_groups=mesh['clip'=2,'ha'=8,'ta'=2] {'ha','ta'}, use_global_device_ids=true, to_apply=%region_2.3 | all-reduce | flops 32 | bytes 256 | tf_op jit(solution)/shard_map/psum | solution.py:109
  66.0 0.3 fusion.2
  66.3 0.1 reduce_sum.37
  66.5 17.1 %psum.22 = f32[32]{0:T(128)S(1)} all-reduce(f32[32]{0:T(128)S(1)} %reduce_sum.37), channel_id=1, replica_groups=mesh['clip'=2,'ha'=8,'ta'=2] {'ha'}, use_global_device_ids=true, to_apply=%region_5.6 | all-reduce | flops 32 | bytes 256 | tf_op jit(solution)/shard_map/psum | solution.py:111
  83.6 2.6 %psum.23 = f32[32]{0:T(128)S(1)} all-reduce(f32[32]{0:T(128)S(1)} %psum.22), channel_id=1, replica_groups=mesh['clip'=2,'ha'=8,'ta'=2] {'ta'}, use_global_device_ids=true, to_apply=%region_6.7 | all-reduce | flops 32 | bytes 256 | tf_op jit(solution)/shard_map/psum | solution.py:111
  86.3 0.1 mul.34
  86.4 1.9 %fusion = bf16[6,4,128,384]{3,2,1,0:T(8,128)(2,1)S(1)} fusion(bf16[6,4,128,384]{3,2,1,0:T(8,128)(2,1)S(1)} %bitcast.53, f32[384]{0:T(512)S(1)} %copy-done.11, f32[384]{0:T(512)S(1)} %copy-done.12, f32[384]{0:T(512)S(1)} %mul.34, f32[384]{0:T(512)S(1)} %sub.26, pred[6,4]{1,0:T(8,128)(4,1)S(1)} %and_and_fusion), kind=kLoop, calls=%fused_computation.5 | loop fusion | flops 12976128 | bytes 4724760 | tf_op jit(solution)/shard_map/jit(_where)/select_n | solution.py:120
  88.3 3.6 %pad_slice_fusion.18 = (bf16[4,2,128,384]{3,2,1,0:T(8,128)(2,1)S(1)}, bf16[4,2,128,384]{3,2,1,0:T(8,128)(2,1)S(1)}, bf16[4,2,128,384]{3,2,1,0:T(8,128)(2,1)S(1)}...) fusion(bf16[6,4,128,384]{3,2,1,0:T(8,128)(2,1)S(1)} %fusion), kind=kLoop, calls=%fused_computation.76 | loop fusion | bytes 13369344 | tf_op jit(solution)/shard_map/slice | solution.py:63
  91.9 0.7 fusion.26
  92.7 3.8 %pad_slice_fusion.19 = (bf16[4,2,128,384]{3,2,1,0:T(8,128)(2,1)S(1)}, bf16[4,2,128,384]{3,2,1,0:T(8,128)(2,1)S(1)}, bf16[4,2,128,384]{3,2,1,0:T(8,128)(2,1)S(1)}...) fusion(bf16[6,4,128,384]{3,2,1,0:T(8,128)(2,1)S(1)} %fusion), kind=kLoop, calls=%fused_computation.77 | loop fusion | bytes 11010048 | tf_op jit(solution)/shard_map/slice | solution.py:63
  96.5 0.3 pad_maximum_fusion.7
  96.8 0.9 copy-done.10
  97.6 1.4 %fusion.34 = f32[1024,384]{1,0:T(8,128)S(1)} fusion(bf16[1024,1152]{1,0:T(8,128)(2,1)S(1)} %bitcast.55, bf16[1152,384]{1,0:T(8,128)(2,1)S(1)} %bitcast.72), kind=kOutput, calls=%fused_computation.103 | convolution fusion | flops 905969664 | bytes 4816896 | tf_op jit(solution)/shard_map/dot_general | solution.py:72
  99.1 0.3 pad_maximum_fusion.6
  99.4 0.9 copy-done.9
  100.3 1.4 %fusion.33 = f32[1024,384]{1,0:T(8,128)S(1)} fusion(bf16[1024,1152]{1,0:T(8,128)(2,1)S(1)} %bitcast.56, bf16[1152,384]{1,0:T(8,128)(2,1)S(1)} %bitcast.71), kind=kOutput, calls=%fused_computation.102 | convolution fusion | flops 905969664 | bytes 4816896 | tf_op jit(solution)/shard_map/dot_general | solution.py:72
  101.7 0.3 pad_maximum_fusion.5
  102.0 0.9 copy-done.8
  102.9 1.4 %fusion.32 = f32[1024,384]{1,0:T(8,128)S(1)} fusion(bf16[1024,1152]{1,0:T(8,128)(2,1)S(1)} %bitcast.57, bf16[1152,384]{1,0:T(8,128)(2,1)S(1)} %bitcast.70), kind=kOutput, calls=%fused_computation.101 | convolution fusion | flops 905969664 | bytes 4816896 | tf_op jit(solution)/shard_map/dot_general | solution.py:72
  104.3 0.3 pad_maximum_fusion.4
  104.6 0.9 copy-done.7
  105.5 1.4 %fusion.31 = f32[1024,384]{1,0:T(8,128)S(1)} fusion(bf16[1024,1152]{1,0:T(8,128)(2,1)S(1)} %bitcast.58, bf16[1152,384]{1,0:T(8,128)(2,1)S(1)} %bitcast.69), kind=kOutput, calls=%fused_computation.100 | convolution fusion | flops 905969664 | bytes 4816896 | tf_op jit(solution)/shard_map/dot_general | solution.py:72
  106.9 0.3 pad_maximum_fusion.3
  107.2 0.9 copy-done.6
  108.1 1.4 %fusion.30 = f32[1024,384]{1,0:T(8,128)S(1)} fusion(bf16[1024,1152]{1,0:T(8,128)(2,1)S(1)} %bitcast.59, bf16[1152,384]{1,0:T(8,128)(2,1)S(1)} %bitcast.68), kind=kOutput, calls=%fused_computation.99 | convolution fusion | flops 905969664 | bytes 4816896 | tf_op jit(solution)/shard_map/dot_general | solution.py:72
  109.5 0.3 pad_maximum_fusion.2
  109.8 0.9 copy-done.5
  110.7 1.4 %fusion.29 = f32[1024,384]{1,0:T(8,128)S(1)} fusion(bf16[1024,1152]{1,0:T(8,128)(2,1)S(1)} %bitcast.60, bf16[1152,384]{1,0:T(8,128)(2,1)S(1)} %bitcast.67), kind=kOutput, calls=%fused_computation.98 | convolution fusion | flops 905969664 | bytes 4816896 | tf_op jit(solution)/shard_map/dot_general | solution.py:72
  112.2 0.3 pad_maximum_fusion
  112.5 0.9 copy-done.4
  113.3 1.4 %fusion.27 = f32[1024,384]{1,0:T(8,128)S(1)} fusion(bf16[1024,1152]{1,0:T(8,128)(2,1)S(1)} %bitcast.61, bf16[1152,384]{1,0:T(8,128)(2,1)S(1)} %bitcast.66), kind=kOutput, calls=%fused_computation.96 | convolution fusion | flops 905969664 | bytes 4816896 | tf_op jit(solution)/shard_map/dot_general | solution.py:72
  114.8 0.3 pad_maximum_fusion.1
  115.1 0.9 copy-done.3
  115.9 1.4 %fusion.28 = f32[1024,384]{1,0:T(8,128)S(1)} fusion(bf16[1024,1152]{1,0:T(8,128)(2,1)S(1)} %bitcast.62, bf16[1152,384]{1,0:T(8,128)(2,1)S(1)} %bitcast.65), kind=kOutput, calls=%fused_computation.97 | convolution fusion | flops 905969664 | bytes 4816896 | tf_op jit(solution)/shard_map/dot_general | solution.py:72
  117.4 0.3 pad_maximum_fusion.8
  117.7 0.9 copy-done.2
  118.5 1.7 %add_add_fusion = f32[1024,384]{1,0:T(8,128)S(1)} fusion(f32[1024,384]{1,0:T(8,128)S(1)} %fusion.34, f32[1024,384]{1,0:T(8,128)S(1)} %fusion.33, f32[1024,384]{1,0:T(8,128)S(1)} %fusion.32, f32[1024,384]{1,0:T(8,128)S(1)} %fusion.31, f32[1024,384]{1,0:T(8,128)S(1)} %fusion.30, f32[1024,384]{1,0:T(8,128)S(1)} %fusion.29, f32[1024,384]{1,0:T(8,128)S(1)} %fusion.27, ...), kind=kOutput, calls=%fused_computation.19 | convolution fusion | flops 909115392 | bytes 17399808 | tf_op jit(solution)/shard_map/dot_general | solution.py:72
  120.3 1.1 fusion.4
  (56 shorter events, 2.1 us)
Async XLA Ops:
  0.0 28.7 %copy-start = (bf16[3,3,3,16,384]{4,3,2,1,0:T(8,128)(2,1)S(1)}, bf16[3,3,3,16,384]{4,3,2,1,0:T(8,128)(2,1)}, u32[]{:S(2)}) copy-start(bf16[3,3,3,16,384]{4,3,2,1,0:T(8,128)(2,1)} %param.8) | copy-start | bytes 995332
  5.3 8.0 %collective-permute-start = (bf16[4,2,128,16]{3,2,1,0:T(8,128)(2,1)S(1)}, bf16[4,2,128,16]{3,2,1,0:T(8,128)(2,1)S(1)}, u32[]{:S(2)}, u32[]{:S(2)}) collective-permute-start(bf16[4,2,128,16]{3,2,1,0:T(8,128)(2,1)S(1)} %bitcast.63), channel_id=1, source_target_pairs={{0,1},{2,3},{4,5},{6,7},{8,9},{10,11},{12,13},{14,15},{16,17},{18,... | collective-permute-start | bytes 98312 | tf_op jit(solution)/shard_map/ppermute | solution.py:15
  13.4 7.1 %collective-permute-start.2 = (bf16[8,2,128,16]{2,3,1,0:T(8,128)(2,1)S(1)}, bf16[8,2,128,16]{2,3,1,0:T(8,128)(2,1)S(1)}, u32[]{:S(2)}, u32[]{:S(2)}) collective-permute-start(bf16[8,2,128,16]{2,3,1,0:T(8,128)(2,1)S(1)} %pad_maximum_fusion.11), channel_id=1, source_target_pairs={{2,0},{4,2},{6,4},{8,6},{10,8},{12,10},{14,12},{3,1},{5,3},{7,5},{... | collective-permute-start | bytes 196616 | tf_op jit(solution)/shard_map/ppermute | solution.py:26
  14.7 7.4 %collective-permute-start.1 = (bf16[8,2,128,16]{2,3,1,0:T(8,128)(2,1)S(1)}, bf16[8,2,128,16]{2,3,1,0:T(8,128)(2,1)S(1)}, u32[]{:S(2)}, u32[]{:S(2)}) collective-permute-start(bf16[8,2,128,16]{2,3,1,0:T(8,128)(2,1)S(1)} %pad_maximum_fusion.11), channel_id=1, source_target_pairs={{0,2},{2,4},{4,6},{6,8},{8,10},{10,12},{12,14},{1,3},{3,5},{5,7},{... | collective-permute-start | bytes 196616 | tf_op jit(solution)/shard_map/ppermute | solution.py:25
  25.5 3.2 %copy-start.14 = (f32[384]{0:T(512)S(1)}, f32[384]{0:T(512)}, u32[]{:S(2)}) copy-start(f32[384]{0:T(512)} %param.9) | copy-start | bytes 4612
  32.3 54.1 %copy-start.11 = (f32[384]{0:T(512)S(1)}, f32[384]{0:T(512)}, u32[]{:S(2)}) copy-start(f32[384]{0:T(512)} %param.11) | copy-start | bytes 4612
  32.3 54.1 %copy-start.12 = (f32[384]{0:T(512)S(1)}, f32[384]{0:T(512)}, u32[]{:S(2)}) copy-start(f32[384]{0:T(512)} %param.10) | copy-start | bytes 4612
  96.5 1.2 copy-start.10
  99.1 1.2 copy-start.9
  101.7 1.2 copy-start.8
  104.3 1.2 copy-start.7
  106.9 1.2 copy-start.6
  109.5 1.2 copy-start.5
  112.1 1.2 copy-start.4
  114.8 1.2 copy-start.3
  117.4 1.2 copy-start.2
  118.5 1.8 %copy-start.13 = (f32[384]{0:T(512)S(1)}, f32[384]{0:T(512)}, u32[]{:S(2)}) copy-start(f32[384]{0:T(512)} %param.13) | copy-start | bytes 4612
  118.5 2.9 %copy-start.1 = (bf16[3,3,3,16,384]{4,3,2,1,0:T(8,128)(2,1)S(1)}, bf16[3,3,3,16,384]{4,3,2,1,0:T(8,128)(2,1)}, u32[]{:S(2)}) copy-start(bf16[3,3,3,16,384]{4,3,2,1,0:T(8,128)(2,1)} %param.8) | copy-start | bytes 995332
